TPU v7x, 8 devices: a whole 2x2x1 slice. The times are simulated.
8 devices in a mesh: dp: 1 (over z), ep: 8 (over y, x, core).
Axes of the slice: x: 2, y: 2, z: 1, core: 2. Of those that a mesh axis runs over, the one named last changes fastest.
Arguments:
- tokens: bfloat16 [16384, 768], P(('dp', 'ep'))
- expert_idx: int32 [16384], P(('dp', 'ep'))
- w_router: float32 [768, 8], replicated
- w_in: bfloat16 [8, 768, 3072], P('ep')
- w_out: bfloat16 [8, 3072, 768], P('ep')
Outputs:
- output: bfloat16 [16384, 768], P(('dp', 'ep'))
All inputs are finite; a program needn't handle non-finite values.
Results may differ from a plain program's by a relative error of at most 0.001.
Values are sent between devices in bfloat16 or wider.
A program may use at most 1 GiB of HBM per device.

v0:
```python
import jax
import jax.numpy as jnp
from jax import lax
from jax.sharding import PartitionSpec as P, NamedSharding


def dispatch(tok_rows, choice, w_router, capacity):
    tok_count = tok_rows.shape[0]
    num_experts = w_router.shape[1]
    logits = jnp.dot(tok_rows.astype(jnp.float32), w_router, precision=lax.Precision.HIGHEST)
    router_prob = jax.nn.softmax(logits, axis=-1)
    chosen = choice[:, None] == jnp.arange(num_experts, dtype=jnp.int32)[None, :]
    gate_prob = jnp.sum(jnp.where(chosen, router_prob, 0.0), axis=-1)
    running_count = jnp.cumsum(chosen.astype(jnp.int32), axis=0) - 1
    position = jnp.sum(jnp.where(chosen, running_count, 0), axis=-1)
    slot_index = jnp.where(position < capacity, choice * capacity + position, num_experts * capacity)
    holder = jnp.full((num_experts * capacity + 1,), tok_count, jnp.int32).at[slot_index].set(jnp.arange(tok_count, dtype=jnp.int32))
    buffer = jnp.take(tok_rows, holder[:-1], axis=0, mode="fill", fill_value=0)
    return buffer, slot_index, gate_prob


def combine(flat_out, slot_index, gate_prob):
    picked = jnp.take(flat_out, slot_index, axis=0, mode="fill", fill_value=0)
    return (gate_prob[:, None] * picked.astype(jnp.float32)).astype(jnp.bfloat16)


def solution(mesh):
    groups = mesh.shape["ep"]

    def local_block(tokens, expert_idx, w_router, w_in, w_out):
        tok_count, model_dim = tokens.shape
        local_experts = w_in.shape[0]
        num_experts = local_experts * groups
        capacity = (5 * tok_count + 4 * num_experts - 1) // (4 * num_experts)
        buffer, slot_index, gate_prob = dispatch(tokens, expert_idx, w_router, capacity)
        send_buf = buffer.reshape(groups, local_experts, capacity, model_dim)
        recv_buf = lax.all_to_all(send_buf, "ep", 0, 2, tiled=True)
        rows_in = recv_buf.reshape(local_experts, groups * capacity, model_dim)
        hidden = jnp.einsum("ecd,edf->ecf", rows_in, w_in, preferred_element_type=jnp.float32)
        hidden_act = jax.nn.relu(hidden).astype(jnp.bfloat16)
        expert_rows = jnp.einsum("ecf,efd->ecd", hidden_act, w_out, preferred_element_type=jnp.float32).astype(jnp.bfloat16)
        back_buf = lax.all_to_all(expert_rows.reshape(1, local_experts, groups * capacity, model_dim), "ep", 2, 0, tiled=True)
        flat_out = back_buf.reshape(num_experts * capacity, model_dim)
        return combine(flat_out, slot_index, gate_prob)

    return jax.shard_map(local_block, mesh=mesh, in_specs=(P(("dp", "ep"), None), P(("dp", "ep")), P(None, None), P("ep", None, None), P("ep", None, None)), out_specs=P(("dp", "ep"), None), check_vma=False)
```

profile of v0, /device:TPU:0, one launch (start us, length us, event | category | flops | bytes accessed | tf_op | source)
XLA Modules:
  0.0 242.6 jit_solution(6990880383819377690)
XLA Ops:
  0.0 0.9 fusion.9
  0.9 2.3 reduce-window.6
  3.1 0.3 slice_reduce_fusion
  3.4 0.2 reduce-window.9
  3.6 0.1 add_bitcast_fusion
  3.7 0.7 fusion.8
  4.4 0.7 fusion.11
  5.1 8.1 %scatter_custom_fusion = s32[2561]{0:T(1024)S(1)} fusion(s32[2048]{0:T(1024)S(1)} %get-tuple-element.6, s32[2048]{0:T(1024)S(1)} %iota.11, s32[]{:T(128)} %constant.31.clone.1), kind=kCustom, calls=%fused_computation.31 | custom fusion | bytes 10248 | tf_op jit(solution)/shard_map/scatter | solution.py:17
  13.2 0.1 slice.14
  13.3 8.6 %gather_fusion = bf16[2560,768]{1,0:T(8,128)(2,1)} fusion(bf16[2048,768]{1,0:T(8,128)(2,1)S(1)} %copy-done, s32[3072]{0:T(1024)S(1)} %pad_clamp_fusion), kind=kCustom, calls=%fused_computation | custom fusion | bytes 7874560 | tf_op jit(solution)/shard_map/jit(_take)/gather | solution.py:18
  21.9 2.4 %broadcast_select_fusion = bf16[8,1,320,768]{3,2,1,0:T(8,128)(2,1)S(1)} fusion(bf16[8,1,320,768]{3,2,1,0:T(8,128)(2,1)} %bitcast.45, pred[8,320]{1,0:T(8,128)(4,1)S(1)} %compare_and_fusion), kind=kLoop, calls=%fused_computation.10 | loop fusion | flops 1966080 | bytes 7866880 | tf_op jit(solution)/shard_map/jit(_take)/select_n | solution.py:18
  24.3 50.3 %all_to_all.8 = bf16[8,1,320,768]{3,2,1,0:T(8,128)(2,1)} all-to-all(bf16[8,1,320,768]{3,2,1,0:T(8,128)(2,1)S(1)} %broadcast_select_fusion), channel_id=1, replica_groups=mesh['dp'=1,'ep'=8] {'ep'}, dimensions={0} | all-to-all | bytes 7864320 | tf_op jit(solution)/shard_map/all_to_all | solution.py:37
  74.7 30.7 %fusion.2 = bf16[1,1,2560,768]{3,2,1,0:T(8,128)(2,1)} fusion(bf16[1,3072,768]{2,1,0:T(8,128)(2,1)} %param.9, bf16[2560,768]{1,0:T(8,128)(2,1)} %bitcast.46, bf16[1,768,3072]{2,1,0:T(8,128)(2,1)} %param.8), kind=kOutput, calls=%fused_computation.8 | convolution fusion | flops 24176885760 | bytes 17301504 | tf_op jit(solution)/shard_map/ecf,efd->ecd/dot_general | solution.py:41
  105.4 8.3 %copy.16 = bf16[1,1,2560,768]{3,1,0,2:T(2,128)(2,1)} copy(bf16[1,1,2560,768]{3,2,1,0:T(8,128)(2,1)} %fusion.2) | data formatting | bytes 7864320 | tf_op jit(solution)/shard_map/reshape | solution.py:42
  113.6 0.5 broadcast.72
  114.2 41.5 %reduce.2 = bf16[2560,768]{1,0:T(8,128)(2,1)} reduce(bf16[2560,1,1,768]{3,2,1,0:T(2,128)(2,1)} %bitcast.43, bf16[]{:T(256)} %broadcast.72), dimensions={1,2}, to_apply=%bitcast.40.reduce_sub_computation | reduce | bytes 7864322
  155.6 6.8 %reshape.119 = bf16[8,2,122880]{2,1,0:T(2,128)(2,1)} reshape(bf16[2560,768]{1,0:T(8,128)(2,1)} %reduce.2) | data formatting | bytes 7864320
  162.5 3.4 %all-to-all-start.1 = ((bf16[8,2,122880]{2,1,0:T(2,128)(2,1)}), bf16[8,2,122880]{2,1,0:T(2,128)(2,1)}, u32[]{:S(2)}, u32[]{:S(2)}) async-start(bf16[8,2,122880]{2,1,0:T(2,128)(2,1)} %reshape.119), calls=%async_computation.1 | async-start | bytes 7864320 | tf_op jit(solution)/shard_map/all_to_all | solution.py:42
  165.9 2.5 %fusion.16 = (f32[2048]{0:T(1024)S(1)}, f32[2048,8]{0,1:T(8,128)S(1)}) fusion(bf16[2048,768]{1,0:T(8,128)(2,1)S(1)} %copy-done, f32[768,8]{0,1:T(8,128)S(1)} %copy-done.2), kind=kOutput, calls=%fused_computation.35 | convolution fusion | flops 151009280 | bytes 3244032 | tf_op jit(solution)/shard_map/dot_general | solution.py:10
  168.5 43.5 %all-to-all-done.1 = bf16[8,2,122880]{2,1,0:T(2,128)(2,1)} async-done(((bf16[8,2,122880]{2,1,0:T(2,128)(2,1)}), bf16[8,2,122880]{2,1,0:T(2,128)(2,1)}, u32[]{:S(2)}, u32[]{:S(2)}) %all-to-all-start.1) | async-done | bytes 3932192 | tf_op jit(solution)/shard_map/all_to_all | solution.py:42
  212.1 8.5 %reshape.120 = bf16[2560,1,1,768]{3,2,1,0:T(2,128)(2,1)} reshape(bf16[8,2,122880]{2,1,0:T(2,128)(2,1)} %all-to-all-done.1) | data formatting | bytes 7864320
  220.5 5.9 %copy.15 = bf16[1,1,2560,768]{3,2,0,1:T(8,128)(2,1)} copy(bf16[1,1,2560,768]{3,1,0,2:T(2,128)(2,1)} %bitcast.44) | data formatting | bytes 7864320
  226.4 12.7 %gather_fusion.1 = bf16[2048,768]{1,0:T(8,128)(2,1)} fusion(bf16[2560,768]{1,0:T(8,128)(2,1)} %bitcast.42, s32[2048]{0:T(1024)S(1)} %get-tuple-element.5), kind=kCustom, calls=%fused_computation.1 | custom fusion | bytes 6299648 | tf_op jit(solution)/shard_map/jit(_take)/gather | solution.py:23
  239.1 3.5 %multiply_convert_fusion = bf16[2048,768]{1,0:T(8,128)(2,1)} fusion(bf16[2048,768]{1,0:T(8,128)(2,1)} %gather_fusion.1, f32[2048]{0:T(1024)S(1)} %select_reduce_fusion, pred[2048]{0:T(1024)(128)(4,1)S(1)} %compare_and_fusion.1), kind=kLoop, calls=%fused_computation.4 | loop fusion | flops 6291456 | bytes 6301696 | tf_op jit(solution)/shard_map/convert_element_type | solution.py:24
  (13 shorter events, 0.1 us)
Async XLA Ops:
  0.0 13.3 %copy-start = (bf16[2048,768]{1,0:T(8,128)(2,1)S(1)}, bf16[2048,768]{1,0:T(8,128)(2,1)}, u32[]{:S(2)}) copy-start(bf16[2048,768]{1,0:T(8,128)(2,1)} %param.5) | copy-start | bytes 9437188
  162.5 3.4 %copy-start.2 = (f32[768,8]{0,1:T(8,128)S(1)}, f32[768,8]{0,1:T(8,128)}, u32[]{:S(2)}) copy-start(f32[768,8]{0,1:T(8,128)} %param.7) | copy-start | bytes 73732
  162.5 6.0 %copy-start.1 = (s32[2048]{0:T(1024)S(1)}, s32[2048]{0:T(1024)}, u32[]{:S(2)}) copy-start(s32[2048]{0:T(1024)} %param.6) | copy-start | bytes 24580
  162.5 49.6 %all-to-all-start.1 = ((bf16[8,2,122880]{2,1,0:T(2,128)(2,1)}), bf16[8,2,122880]{2,1,0:T(2,128)(2,1)}, u32[]{:S(2)}, u32[]{:S(2)}) async-start(bf16[8,2,122880]{2,1,0:T(2,128)(2,1)} %reshape.119), calls=%async_computation.1 | async-start | bytes 7864320 | tf_op jit(solution)/shard_map/all_to_all | solution.py:42
where the time goes:
time: 243 us
  local copies, waits for them, and re-layouts  59.6 us (25%)
  other arithmetic  52.4 us (22%)
  blocking collectives  50.3 us (21%)
  waiting for transfers between devices  43.5 us (18%)
  matrix products  33.2 us (14%)
  starting transfers between devices  3.4 us (1%)
    all_to_all x1, blocking collectives, local_block(): recv_buf = lax.all_to_all(send_buf, 'ep', 0, 2, tiled=True)  50.3 us
    all_to_all x1, waiting for transfers between devices, local_block(): lax.all_to_all(expert_rows.reshape(1, local_experts, groups * capacity, m...  43.5 us
    unnamed x2, other arithmetic  41.6 us
    dot_general x1, matrix products, local_block(): jnp.einsum('ecf,efd->ecd', hidden_act, w_out, preferred_element_type=jnp....  30.7 us
    unnamed x10, local copies, waits for them, and re-layouts  21.7 us
    gather x1, local copies, waits for them, and re-layouts, combine(): picked = jnp.take(flat_out, slot_index, axis=0, mode='fill', fill_value=0)  12.7 us
    gather x1, local copies, waits for them, and re-layouts, dispatch(): buffer = jnp.take(tok_rows, holder[:-1], axis=0, mode='fill', fill_value=0)  8.56 us
    reshape x1, local copies, waits for them, and re-layouts, local_block(): expert_rows.reshape(1, local_experts, groups * capacity, model_dim)  8.28 us
  transfers between devices with their start and end apart: 1, of which 1 were waited for; matrix products, arithmetic and copies ran while one was open for 1% of the time, Pallas kernels for 0%

commit v1 on v0

v1 whole, which is shorter than its diff:
```python
import functools

import jax
import jax.numpy as jnp
from jax import lax
from jax.experimental import pallas as pl
from jax.experimental.pallas import tpu as pltpu
from jax.sharding import PartitionSpec as P

MESH = pl.DeviceIdType.MESH
LANES = 128
F32 = jnp.float32
BF16 = jnp.bfloat16

SEND_ORDER = (6, 7, 2, 4, 3, 5, 1, 0)
WORK_ORDER = (0, 1, 6, 7, 2, 4, 3, 5)


def packed(order):
    return sum(k * 8**i for i, k in enumerate(order))


def partner(me, k):
    core = lax.rem(lax.rem(me, 2) + lax.rem(k, 2), 2)
    along_x = lax.rem(lax.rem(me // 2, 2) + lax.rem(k // 2, 2), 2)
    along_y = lax.rem(me // 4 + k // 4, 2)
    return along_y * 4 + along_x * 2 + core


def kernel(capacity, num_experts, x_hbm, idx_hbm, wr_hbm, w_in_hbm, w_out_hbm, y_hbm,
           x, idx, wr, w_in, w_out, onehot, hidden, code_rows, gate_rows, code_cols, gate_cols, acc,
           sent, recv, back, home, load_sem, store_sem, send_sem, recv_sem, back_sem, home_sem):
    me = lax.axis_index("ep")
    tokens, model_dim = x.shape
    hidden_dim = w_in.shape[1]
    tiles = tokens // LANES

    loads = [pltpu.make_async_copy(src, dst, load_sem.at[i]) for i, (src, dst) in enumerate(
        ((idx_hbm, idx), (x_hbm, x), (wr_hbm, wr), (w_in_hbm, w_in), (w_out_hbm, w_out)))]
    for load in loads:
        load.start()
    barrier = pltpu.get_barrier_semaphore()
    for k in range(1, num_experts):
        pl.semaphore_signal(barrier, inc=1, device_id={"ep": partner(me, k)}, device_id_type=MESH)

    def outward(k):
        return pltpu.make_async_remote_copy(sent.at[k], recv.at[k], send_sem.at[k], recv_sem.at[k], device_id={"ep": partner(me, k)}, device_id_type=MESH)

    def homeward(k):
        return pltpu.make_async_remote_copy(back.at[k], home.at[k], back_sem.at[k], home_sem.at[k], device_id={"ep": partner(me, k)}, device_id_type=MESH)

    loads[0].wait()
    choice = idx[...]
    rows = num_experts * tiles
    chosen = jnp.concatenate([(choice == e).astype(F32) for e in range(num_experts)], axis=0)
    row = lax.broadcasted_iota(jnp.int32, (rows, rows), 0)
    col = lax.broadcasted_iota(jnp.int32, (rows, rows), 1)
    earlier_tile = ((row // tiles == col // tiles) & (col < row)).astype(BF16)
    lane_row = lax.broadcasted_iota(jnp.int32, (LANES, LANES), 0)
    lane_col = lax.broadcasted_iota(jnp.int32, (LANES, LANES), 1)
    up_to = (lane_row <= lane_col).astype(BF16)
    chosen16 = chosen.astype(BF16)
    inside = jnp.dot(chosen16, up_to, preferred_element_type=F32)
    before = jnp.dot(earlier_tile, chosen16, preferred_element_type=F32)
    before = jnp.dot(before.astype(BF16), jnp.ones((LANES, LANES), BF16), preferred_element_type=F32)
    count = chosen * (inside + before)
    position = count[:tiles]
    for e in range(1, num_experts):
        position = position + count[e * tiles:(e + 1) * tiles]
    position = position.astype(jnp.int32) - 1
    code = jnp.where(position < capacity, choice * capacity + position, -(2**20))
    code_rows[...] = code

    loads[1].wait()

    def dispatch(step, order):
        k = lax.rem(order, 8)
        first = partner(me, k) * capacity
        slot = lax.broadcasted_iota(jnp.int32, (capacity, LANES), 0) + first
        for i in range(tiles):
            onehot[:, i * LANES:(i + 1) * LANES] = (slot == code_rows[i:i + 1, :]).astype(F32).astype(BF16)
        picked = jnp.dot(onehot[...], x[...], preferred_element_type=F32).astype(BF16)

        @pl.when(step < num_experts - 1)
        def _():
            sent[k] = picked

            @pl.when(step == 0)
            def _():
                pl.semaphore_wait(barrier, num_experts - 1)
            outward(k).start()

        @pl.when(step == num_experts - 1)
        def _():
            recv[0] = picked
        return order // 8

    lax.fori_loop(0, num_experts, dispatch, packed(SEND_ORDER))

    loads[2].wait()
    weight = wr[...]
    high = weight.astype(BF16)
    rest = weight - high.astype(F32)
    mid = rest.astype(BF16)
    low = (rest - mid.astype(F32)).astype(BF16)
    parts = [lax.dot_general(part, x[...], (((1,), (1,)), ((), ())), preferred_element_type=F32) for part in (low, mid, high)]
    logits = parts[0] + parts[1] + parts[2]
    top = jnp.max(logits, axis=0, keepdims=True)
    grown = jnp.exp(logits - top)
    total = jnp.sum(grown, axis=0, keepdims=True)
    prob = grown / total
    expert = lax.broadcasted_iota(jnp.int32, (num_experts, LANES), 0)
    for i in range(tiles):
        mine = expert == idx[i:i + 1, :]
        gate_rows[i:i + 1, :] = jnp.sum(jnp.where(mine, prob[:, i * LANES:(i + 1) * LANES], 0.0), axis=0, keepdims=True)
    pad = jnp.zeros((LANES - tiles, LANES), F32)
    code_t = jnp.concatenate([code_rows[...].astype(F32), pad], axis=0).T
    gate_t = jnp.concatenate([gate_rows[...], pad], axis=0).T
    for i in range(tiles):
        code_cols[i * LANES:(i + 1) * LANES, :] = jnp.broadcast_to(code_t[:, i:i + 1], (LANES, LANES)).astype(jnp.int32)
        gate_cols[i * LANES:(i + 1) * LANES, :] = jnp.broadcast_to(gate_t[:, i:i + 1], (LANES, LANES))

    loads[3].wait()
    loads[4].wait()
    chunk = hidden_dim // 3

    def expert_step(step, order):
        k = lax.rem(order, 8)

        @pl.when(step > 0)
        def _():
            outward(k).wait_recv()

        def up(n, carry):
            cols = pl.ds(pl.multiple_of(n * chunk, chunk), chunk)
            part = jnp.dot(recv[k], w_in[:, cols], preferred_element_type=F32)
            hidden[:, cols] = jnp.maximum(part, 0.0).astype(BF16)
            return carry

        lax.fori_loop(0, 3, up, 0)
        result = jnp.dot(hidden[...], w_out[...], preferred_element_type=F32).astype(BF16)

        @pl.when(step > 0)
        def _():
            back[k] = result
            homeward(k).start()

        @pl.when(step == 0)
        def _():
            home[0] = result
        return order // 8

    lax.fori_loop(0, num_experts, expert_step, packed(WORK_ORDER))

    tile = 256
    lane = lax.broadcasted_iota(jnp.int32, (tile, LANES), 1)
    lane_blocks = -(-capacity // LANES)

    def gathered(k, at):
        offset = code_cols[at, :] - partner(me, k) * capacity
        pick = jnp.concatenate([(offset == lane + b * LANES).astype(F32).astype(BF16) for b in range(lane_blocks)], axis=1)
        return jnp.dot(pick[:, :capacity], home[k], preferred_element_type=F32)

    def at_tile(t):
        return pl.ds(pl.multiple_of(t * tile, tile), tile)

    def combine(step, order):
        k = lax.rem(order, 8)

        @pl.when(step > 0)
        def _():
            homeward(k).wait_recv()

        def on_tile(t, carry):
            acc[at_tile(t), :] = (acc[at_tile(t), :].astype(F32) + gathered(k, at_tile(t))).astype(BF16)
            return carry

        lax.fori_loop(0, tokens // tile, on_tile, 0)
        return order // 8

    acc[...] = jnp.zeros_like(acc)
    lax.fori_loop(0, num_experts - 1, combine, packed(WORK_ORDER))
    last = WORK_ORDER[-1]
    homeward(last).wait_recv()

    def store(t):
        return pltpu.make_async_copy(acc.at[at_tile(t), :], y_hbm.at[at_tile(t), :], store_sem.at[t])

    def finish(t, carry):
        value = acc[at_tile(t), :].astype(F32) + gathered(last, at_tile(t))
        for b in range(model_dim // LANES):
            lanes = slice(b * LANES, (b + 1) * LANES)
            acc[at_tile(t), lanes] = (gate_cols[at_tile(t), :] * value[:, lanes]).astype(BF16)
        store(t).start()
        return carry

    lax.fori_loop(0, tokens // tile, finish, 0)
    for k in range(1, num_experts):
        outward(k).wait_send()
        homeward(k).wait_send()
    for t in range(tokens // tile):
        store(t).wait()


def solution(mesh):
    def local_block(tokens, expert_idx, w_router, w_in, w_out):
        tok_count, model_dim = tokens.shape
        local_experts, _, hidden_dim = w_in.shape
        num_experts = w_router.shape[1]
        capacity = (5 * tok_count + 4 * num_experts - 1) // (4 * num_experts)
        tiles = tok_count // LANES
        blocks = (num_experts, capacity, model_dim)
        anywhere = pl.BlockSpec(memory_space=pl.ANY)
        return pl.pallas_call(
            functools.partial(kernel, capacity, num_experts),
            out_shape=jax.ShapeDtypeStruct((tok_count, model_dim), BF16),
            in_specs=[anywhere] * 5,
            out_specs=anywhere,
            scratch_shapes=[
                pltpu.VMEM((tok_count, model_dim), BF16),
                pltpu.VMEM((tiles, LANES), jnp.int32),
                pltpu.VMEM((num_experts, model_dim), F32),
                pltpu.VMEM((model_dim, hidden_dim), BF16),
                pltpu.VMEM((hidden_dim, model_dim), BF16),
                pltpu.VMEM((capacity, tok_count), BF16),
                pltpu.VMEM((capacity, hidden_dim), BF16),
                pltpu.VMEM((tiles, LANES), jnp.int32),
                pltpu.VMEM((tiles, LANES), F32),
                pltpu.VMEM((tok_count, LANES), jnp.int32),
                pltpu.VMEM((tok_count, LANES), F32),
                pltpu.VMEM((tok_count, model_dim), BF16),
                pltpu.VMEM(blocks, BF16),
                pltpu.VMEM(blocks, BF16),
                pltpu.VMEM(blocks, BF16),
                pltpu.VMEM(blocks, BF16),
                pltpu.SemaphoreType.DMA((5,)),
                pltpu.SemaphoreType.DMA((tok_count // 256,)),
                pltpu.SemaphoreType.DMA((num_experts,)),
                pltpu.SemaphoreType.DMA((num_experts,)),
                pltpu.SemaphoreType.DMA((num_experts,)),
                pltpu.SemaphoreType.DMA((num_experts,)),
            ],
            compiler_params=pltpu.CompilerParams(collective_id=0, has_side_effects=True, vmem_limit_bytes=62 * 2**20),
            name="moe",
        )(tokens, expert_idx.reshape(tiles, LANES), w_router.T, w_in.reshape(model_dim, hidden_dim), w_out.reshape(hidden_dim, model_dim))

    return jax.shard_map(local_block, mesh=mesh, in_specs=(P(("dp", "ep"), None), P(("dp", "ep")), P(None, None), P("ep", None, None), P("ep", None, None)), out_specs=P(("dp", "ep"), None), check_vma=False)
```

time: 243 us -> 102 us (0.42)
  the two profiles are of different devices: /device:TPU:0 before, /device:TPU:1 now
where the time goes in v1:
time: 102 us
  Pallas kernels  97.9 us (96%)
  local copies, waits for them, and re-layouts  3.76 us (4%)
    pallas_call x1, Pallas kernels, local_block(): pl.pallas_call(functools.partial(kernel, capacity, num_experts), out_shap...  97.9 us
    unnamed x1, local copies, waits for them, and re-layouts  3.76 us

profile of v1, /device:TPU:1, one launch (start us, length us, event | category | flops | bytes accessed | tf_op | source)
XLA Modules:
  0.0 101.7 jit_solution(8267781964387787348)
XLA Ops:
  0.0 97.9 %moe.1 = bf16[2048,768]{1,0:T(8,128)(2,1)} custom-call(bf16[2048,768]{1,0:T(8,128)(2,1)} %x_hbm.1, s32[16,128]{1,0:T(8,128)} %bitcast.7, f32[8,768]{1,0:T(8,128)} %bitcast.6, bf16[768,3072]{1,0:T(8,128)(2,1)} %bitcast.4, bf16[3072,768]{1,0:T(8,128)(2,1)} %bitcast.5), custom_call_target="tpu_custom_call" | custom-call | tf_op jit(solution)/shard_map/moe/pallas_call | solution.py:214
  97.9 3.8 %copy.7 = bf16[2048,768]{1,0:T(8,128)(2,1)} copy(bf16[2048,768]{1,0:T(8,128)(2,1)} %moe.1) | data formatting | bytes 6291456

commit v2 on v1

v2 whole, which is shorter than its diff:
```python
import functools

import jax
import jax.numpy as jnp
from jax import lax
from jax.experimental import pallas as pl
from jax.experimental.pallas import tpu as pltpu
from jax.sharding import PartitionSpec as P

MESH = pl.DeviceIdType.MESH
LANES = 128
F32 = jnp.float32
BF16 = jnp.bfloat16

PARTNERS = (0, 1, 6, 7, 2, 4, 3, 5)
REMOTE_FIRST = (2, 3, 4, 5, 6, 7, 1, 0)


def packed(order):
    return sum(k * 8**i for i, k in enumerate(order))


def partner(me, k):
    core = lax.rem(lax.rem(me, 2) + lax.rem(k, 2), 2)
    along_x = lax.rem(lax.rem(me // 2, 2) + lax.rem(k // 2, 2), 2)
    along_y = lax.rem(me // 4 + k // 4, 2)
    return along_y * 4 + along_x * 2 + core


def kernel(capacity, num_experts, x_hbm, idx_hbm, wr_hbm, w_in_hbm, w_out_hbm, y,
           x, idx, wr, w_in, w_out, onehot, hidden, code_rows, gate_rows, code_cols, gate_cols,
           sent, recv, back, home, tail, load_sem, send_sem, recv_sem, back_sem, home_sem):
    me = lax.axis_index("ep")
    tokens, model_dim = x.shape
    hidden_dim = w_in.shape[1]
    tiles = tokens // LANES
    half = capacity // 2
    main = home.shape[1]
    rest = tail.shape[1]

    load_idx, load_x, load_wr, load_in, load_out = [pltpu.make_async_copy(src, dst, load_sem.at[i]) for i, (src, dst) in enumerate(
        ((idx_hbm, idx), (x_hbm, x), (wr_hbm, wr), (w_in_hbm, w_in), (w_out_hbm, w_out)))]
    load_idx.start()
    load_x.start()
    load_wr.start()
    barrier = pltpu.get_barrier_semaphore()
    for k in range(1, num_experts):
        pl.semaphore_signal(barrier, inc=1, device_id={"ep": partner(me, k)}, device_id_type=MESH)

    def remote(src, dst, sem_a, sem_b, k):
        return pltpu.make_async_remote_copy(src, dst, sem_a, sem_b, device_id={"ep": partner(me, k)}, device_id_type=MESH)

    def outward(s, h, k):
        rows = pl.ds(pl.multiple_of(h * half, half), half)
        return remote(sent.at[s, rows], recv.at[s, rows], send_sem.at[s, h], recv_sem.at[s, h], k)

    def homeward(s, k):
        return remote(back.at[s, :main], home.at[s], back_sem.at[s, 0], home_sem.at[s, 0], k)

    def homeward_rest(s, k):
        return remote(back.at[s, main:], tail.at[s], back_sem.at[s, 1], home_sem.at[s, 1], k)

    load_idx.wait()
    choice = idx[...]
    chosen = jnp.concatenate([(choice == partner(me, k)).astype(F32) for k in PARTNERS], axis=0)
    rows = num_experts * tiles
    row = lax.broadcasted_iota(jnp.int32, (rows, rows), 0)
    col = lax.broadcasted_iota(jnp.int32, (rows, rows), 1)
    earlier_tile = ((row // tiles == col // tiles) & (col < row)).astype(BF16)
    lane_row = lax.broadcasted_iota(jnp.int32, (LANES, LANES), 0)
    lane_col = lax.broadcasted_iota(jnp.int32, (LANES, LANES), 1)
    up_to = (lane_row <= lane_col).astype(BF16)
    chosen16 = chosen.astype(BF16)
    inside = jnp.dot(chosen16, up_to, preferred_element_type=F32)
    before = jnp.dot(earlier_tile, chosen16, preferred_element_type=F32)
    before = jnp.dot(before.astype(BF16), jnp.ones((LANES, LANES), BF16), preferred_element_type=F32)
    position = (inside + before).astype(jnp.int32) - 1
    code = jnp.full((tiles, LANES), -1, jnp.int32)
    for s in range(num_experts):
        at = slice(s * tiles, (s + 1) * tiles)
        code = jnp.where((chosen[at] > 0.0) & (position[at] < capacity), position[at] + s * capacity, code)
    code_rows[...] = code

    load_x.wait()
    load_in.start()
    load_out.start()

    def dispatch(step, carry):
        steps, order = carry
        s, k, h = lax.rem(steps, 8), lax.rem(order, 8), lax.rem(step, 2)
        slot = lax.broadcasted_iota(jnp.int32, (half, LANES), 0) + (s * capacity + h * half)
        for i in range(tiles):
            onehot[:, i * LANES:(i + 1) * LANES] = (slot == code_rows[i:i + 1, :]).astype(F32).astype(BF16)
        picked = jnp.dot(onehot[...], x[...], preferred_element_type=F32).astype(BF16)
        there = pl.ds(pl.multiple_of(h * half, half), half)

        @pl.when(step < 2 * num_experts - 2)
        def _():
            sent[s, there] = picked

            @pl.when(step == 0)
            def _():
                pl.semaphore_wait(barrier, num_experts - 1)
            outward(s, h, k).start()

        @pl.when(step >= 2 * num_experts - 2)
        def _():
            recv[0, there] = picked
        return jnp.where(h == 1, steps // 8, steps), jnp.where(h == 1, order // 8, order)

    lax.fori_loop(0, 2 * num_experts, dispatch, (packed(REMOTE_FIRST), packed([PARTNERS[s] for s in REMOTE_FIRST])))

    load_wr.wait()
    weight = wr[...]
    high = weight.astype(BF16)
    left = weight - high.astype(F32)
    mid = left.astype(BF16)
    low = (left - mid.astype(F32)).astype(BF16)
    parts = [lax.dot_general(part, x[...], (((1,), (1,)), ((), ())), preferred_element_type=F32) for part in (low, mid, high)]
    logits = parts[0] + parts[1] + parts[2]
    top = jnp.max(logits, axis=0, keepdims=True)
    grown = jnp.exp(logits - top)
    total = jnp.sum(grown, axis=0, keepdims=True)
    prob = grown / total
    expert = lax.broadcasted_iota(jnp.int32, (num_experts, LANES), 0)
    for i in range(tiles):
        mine = expert == idx[i:i + 1, :]
        gate_rows[i:i + 1, :] = jnp.sum(jnp.where(mine, prob[:, i * LANES:(i + 1) * LANES], 0.0), axis=0, keepdims=True)
    pad = jnp.zeros((LANES - tiles, LANES), F32)
    code_t = jnp.concatenate([code_rows[...].astype(F32), pad], axis=0).T
    gate_t = jnp.concatenate([gate_rows[...], pad], axis=0).T
    for i in range(tiles):
        code_cols[i * LANES:(i + 1) * LANES, :] = jnp.broadcast_to(code_t[:, i:i + 1], (LANES, LANES)).astype(jnp.int32)
        gate_cols[i * LANES:(i + 1) * LANES, :] = jnp.broadcast_to(gate_t[:, i:i + 1], (LANES, LANES))

    load_in.wait()
    load_out.wait()
    chunk = hidden_dim // 3

    def expert_step(s, order):
        k = lax.rem(order, 8)

        @pl.when(s > 0)
        def _():
            outward(s, 0, k).wait_recv()
            outward(s, 1, k).wait_recv()

        def up(n, carry):
            cols = pl.ds(pl.multiple_of(n * chunk, chunk), chunk)
            part = jnp.dot(recv[s], w_in[:, cols], preferred_element_type=F32)
            hidden[:, cols] = jnp.maximum(part, 0.0).astype(BF16)
            return carry

        lax.fori_loop(0, 3, up, 0)
        result = jnp.dot(hidden[...], w_out[...], preferred_element_type=F32).astype(BF16)

        @pl.when(s > 0)
        def _():
            back[s] = result
            homeward(s, k).start()
            homeward_rest(s, k).start()

        @pl.when(s == 0)
        def _():
            home[0] = result[:main]
            tail[0] = result[main:]
        return order // 8

    lax.fori_loop(0, num_experts, expert_step, packed(PARTNERS))

    tile = 512
    lane = lax.broadcasted_iota(jnp.int32, (1, LANES), 1)

    def gathered(at, targets, block):
        pick = jnp.concatenate([(code_cols[at, :] == target).astype(F32).astype(BF16) for target in targets], axis=1)
        return jnp.dot(pick, block, preferred_element_type=F32)

    def at_tile(t):
        return pl.ds(pl.multiple_of(t * tile, tile), tile)

    def add(targets, block):
        def on_tile(t, carry):
            y[at_tile(t), :] = y[at_tile(t), :] + gathered(at_tile(t), targets, block).astype(BF16)
            return carry
        lax.fori_loop(0, tokens // tile, on_tile, 0)

    def combine(s, order):
        k = lax.rem(order, 8)

        @pl.when(s > 0)
        def _():
            homeward(s, k).wait_recv()
        add([lane + (s * capacity + b * LANES) for b in range(main // LANES)], home[s])
        return order // 8

    def rest_targets(first):
        out = []
        for b in range(2):
            within = lane + b * LANES
            out.append((first + within // rest) * capacity + main + lax.rem(within, rest))
        return out

    y[...] = jnp.zeros_like(y)
    split = num_experts - 2
    lax.fori_loop(0, split, combine, packed(PARTNERS[:split]))
    count = 2 * LANES // rest
    for s in range(1, count):
        homeward_rest(s, PARTNERS[s]).wait_recv()
    add(rest_targets(0), tail[:count].reshape(2 * LANES, model_dim))
    lax.fori_loop(split, num_experts, combine, packed(PARTNERS[split:]))
    for s in range(count, num_experts):
        homeward_rest(s, PARTNERS[s]).wait_recv()

    def finish(t, carry):
        value = y[at_tile(t), :].astype(F32) + gathered(at_tile(t), rest_targets(count), tail[count:].reshape(2 * LANES, model_dim))
        for b in range(model_dim // LANES):
            lanes = slice(b * LANES, (b + 1) * LANES)
            y[at_tile(t), lanes] = (gate_cols[at_tile(t), :] * value[:, lanes]).astype(BF16)
        return carry

    lax.fori_loop(0, tokens // tile, finish, 0)
    for s in range(1, num_experts):
        outward(s, 0, PARTNERS[s]).wait_send()
        outward(s, 1, PARTNERS[s]).wait_send()
        homeward(s, PARTNERS[s]).wait_send()
        homeward_rest(s, PARTNERS[s]).wait_send()


def solution(mesh):
    def local_block(tokens, expert_idx, w_router, w_in, w_out):
        tok_count, model_dim = tokens.shape
        local_experts, _, hidden_dim = w_in.shape
        num_experts = w_router.shape[1]
        capacity = (5 * tok_count + 4 * num_experts - 1) // (4 * num_experts)
        tiles = tok_count // LANES
        main = 2 * LANES
        in_hbm = pl.BlockSpec(memory_space=pltpu.HBM)
        return pl.pallas_call(
            functools.partial(kernel, capacity, num_experts),
            out_shape=pltpu.VMEM((tok_count, model_dim), BF16),
            in_specs=[in_hbm] * 5,
            out_specs=pl.BlockSpec(memory_space=pltpu.VMEM),
            scratch_shapes=[
                pltpu.VMEM((tok_count, model_dim), BF16),
                pltpu.VMEM((tiles, LANES), jnp.int32),
                pltpu.VMEM((num_experts, model_dim), F32),
                pltpu.VMEM((model_dim, hidden_dim), BF16),
                pltpu.VMEM((hidden_dim, model_dim), BF16),
                pltpu.VMEM((capacity // 2, tok_count), BF16),
                pltpu.VMEM((capacity, hidden_dim), BF16),
                pltpu.VMEM((tiles, LANES), jnp.int32),
                pltpu.VMEM((tiles, LANES), F32),
                pltpu.VMEM((tok_count, LANES), jnp.int32),
                pltpu.VMEM((tok_count, LANES), F32),
                pltpu.VMEM((num_experts, capacity, model_dim), BF16),
                pltpu.VMEM((num_experts, capacity, model_dim), BF16),
                pltpu.VMEM((num_experts, capacity, model_dim), BF16),
                pltpu.VMEM((num_experts, main, model_dim), BF16),
                pltpu.VMEM((num_experts, capacity - main, model_dim), BF16),
                pltpu.SemaphoreType.DMA((5,)),
                pltpu.SemaphoreType.DMA((num_experts, 2)),
                pltpu.SemaphoreType.DMA((num_experts, 2)),
                pltpu.SemaphoreType.DMA((num_experts, 2)),
                pltpu.SemaphoreType.DMA((num_experts, 2)),
            ],
            compiler_params=pltpu.CompilerParams(collective_id=0, has_side_effects=True, vmem_limit_bytes=48 * 2**20),
            name="moe",
        )(*[pltpu.with_memory_space_constraint(a, pltpu.HBM) for a in (
            tokens, expert_idx.reshape(tiles, LANES), w_router.T, w_in.reshape(model_dim, hidden_dim), w_out.reshape(hidden_dim, model_dim))])

    return jax.shard_map(local_block, mesh=mesh, in_specs=(P(("dp", "ep"), None), P(("dp", "ep")), P(None, None), P("ep", None, None), P("ep", None, None)), out_specs=P(("dp", "ep"), None), check_vma=False)
```

time: 102 us -> 96.2 us (0.943)
  Pallas kernels: 97.9 us -> 94.4 us
  local copies, waits for them, and re-layouts: 3.76 us -> 1.67 us
    pallas_call x1, Pallas kernels: 97.9 us -> 94.4 us  [local_block(): pl.pallas_call(functools.partial(kernel, capacity, num_experts), out_shap...]
    unnamed x1, local copies, waits for them, and re-layouts: 3.76 us -> 1.67 us
where the time goes in v2:
time: 96.2 us; the launch traced here: 96.1 us
  Pallas kernels  94.4 us (98%)
  local copies, waits for them, and re-layouts  1.67 us (2%)
    pallas_call x1, Pallas kernels, local_block(): pl.pallas_call(functools.partial(kernel, capacity, num_experts), out_shap...  94.4 us

profile of v2, /device:TPU:1, one launch (start us, length us, event | category | flops | bytes accessed | tf_op | source)
XLA Modules:
  0.0 96.1 jit_solution(7222207740259148457)
XLA Ops:
  0.0 94.4 %moe.1 = bf16[2048,768]{1,0:T(8,128)(2,1)S(1)} custom-call(bf16[2048,768]{1,0:T(8,128)(2,1)} %x_hbm.1, s32[16,128]{1,0:T(8,128)} %bitcast.7, f32[8,768]{1,0:T(8,128)} %bitcast.6, bf16[768,3072]{1,0:T(8,128)(2,1)} %bitcast.4, bf16[3072,768]{1,0:T(8,128)(2,1)} %bitcast.5), custom_call_target="tpu_custom_call" | custom-call | tf_op jit(solution)/shard_map/moe/pallas_call | solution.py:238
  94.4 1.7 %copy.7 = bf16[2048,768]{1,0:T(8,128)(2,1)} copy(bf16[2048,768]{1,0:T(8,128)(2,1)S(1)} %moe.1) | data formatting | bytes 6291456
